TPU v7x, 32 devices: a whole 2x2x4 slice. The times are simulated.
32 devices in a mesh: rep: 1, dp: 32 (over x, y, z, core).
Axes of the slice: x: 2, y: 2, z: 4, core: 2. Of those that a mesh axis runs over, the one named last changes fastest.
Arguments:
- g_w_gate: bfloat16 [32, 2, 512, 8192], P(('rep', 'dp'))
- g_w_up: bfloat16 [32, 2, 512, 8192], P(('rep', 'dp'))
- g_w_down: bfloat16 [32, 2, 8192, 512], P(('rep', 'dp'))
- w_gate: bfloat16 [2, 512, 8192], replicated
- w_up: bfloat16 [2, 512, 8192], replicated
- w_down: bfloat16 [2, 8192, 512], replicated
- m_w_gate: float32 [2, 512, 8192], P(None, 'dp')
- m_w_up: float32 [2, 512, 8192], P(None, 'dp')
- m_w_down: float32 [2, 8192, 512], P(None, 'dp')
- v_w_gate: float32 [2, 512, 8192], P(None, 'dp')
- v_w_up: float32 [2, 512, 8192], P(None, 'dp')
- v_w_down: float32 [2, 8192, 512], P(None, 'dp')
Outputs:
- output 1: bfloat16 [2, 512, 8192], P('rep')
- output 2: bfloat16 [2, 512, 8192], P('rep')
- output 3: bfloat16 [2, 8192, 512], P('rep')
- output 4: float32 [2, 512, 8192], P('rep', 'dp')
- output 5: float32 [2, 512, 8192], P('rep', 'dp')
- output 6: float32 [2, 8192, 512], P('rep', 'dp')
- output 7: float32 [2, 512, 8192], P('rep', 'dp')
- output 8: float32 [2, 512, 8192], P('rep', 'dp')
- output 9: float32 [2, 8192, 512], P('rep', 'dp')
All inputs are finite; a program needn't handle non-finite values.
Results may differ from a plain program's by a relative error of at most 0.022.
Values are sent between devices in bfloat16 or wider.
A program may use at most 2 GiB of HBM per device.

v0:
```python
import jax
import jax.numpy as jnp
from jax import lax
from jax.sharding import PartitionSpec as P


def adamw(w, m, v, g):
    m = 0.9 * m + 0.1 * g
    v = 0.95 * v + 0.05 * g * g
    step = m * lax.rsqrt(v + 1e-8) + 0.1 * w
    return (w - 0.02 * step).astype(jnp.bfloat16), m, v


def solution(mesh):
    def step(*arrays):
        terms, weights, m, v = (arrays[i : i + 3] for i in (0, 3, 6, 9))
        gradients = [lax.psum_scatter(t[0], "dp", scatter_dimension=1, tiled=True).astype(jnp.float32) for t in terms]
        me = lax.axis_index("dp")
        own = [lax.dynamic_slice_in_dim(w, me * one.shape[1], one.shape[1], 1).astype(jnp.float32) for w, one in zip(weights, m, strict=True)]
        new = [adamw(w, m, v, g) for w, m, v, g in zip(own, m, v, gradients, strict=True)]
        whole = [lax.all_gather(one[0], "dp", axis=1, tiled=True) for one in new]
        return (*whole, *(one[1] for one in new), *(one[2] for one in new))

    all_of, cut = P(None, None, None), P(None, "dp", None)
    return jax.shard_map(
        step,
        mesh=mesh,
        in_specs=(P(("rep", "dp"), None, None, None),) * 3 + (all_of,) * 3 + (cut,) * 6,
        out_specs=(P("rep", None, None),) * 3 + (P("rep", "dp", None),) * 6,
        check_vma=False,
    )
```

profile of v0, /device:TPU:0, one launch (start us, length us, event | category | flops | bytes accessed | tf_op | source)
XLA Modules:
  0.0 960.5 jit_solution(17940469044486142106)
XLA Ops:
  7.2 0.0 reduce-scatter.8.cloned.1.call-start
  7.2 0.7 reduce-scatter.8.cloned.1.call-update
  7.9 0.0 reduce-scatter.6.cloned.1.call-start
  8.0 0.7 reduce-scatter.6.cloned.1.call-update
  8.7 0.0 reduce-scatter.4.cloned.1.call-start
  8.7 0.7 reduce-scatter.4.cloned.1.call-update
  9.4 0.0 all-gather.8.cloned.1.call-start
  9.4 190.0 %reduce-scatter.8.cloned.1.call-done = bf16[2,256,512]{2,1,0:T(8,128)(2,1)} async-done(((bf16[2,8192,512]{2,1,0:T(8,128)(2,1)}), bf16[2,256,512]{2,1,0:T(8,128)(2,1)}) %reduce-scatter.8.cloned.1.call-update) | async-done | bytes 524304 | tf_op jit(solution)/shard_map/reduce_scatter | solution.py:17
  199.4 3.0 fusion.10
  202.5 0.0 all-gather.8.cloned.1.call-update
  202.5 0.0 all-gather.6.cloned.1.call-start
  202.5 183.4 %reduce-scatter.6.cloned.1.call-done = bf16[2,16,8192]{2,1,0:T(8,128)(2,1)} async-done(((bf16[2,512,8192]{2,1,0:T(8,128)(2,1)}), bf16[2,16,8192]{2,1,0:T(8,128)(2,1)}) %reduce-scatter.6.cloned.1.call-update) | async-done | bytes 524304 | tf_op jit(solution)/shard_map/reduce_scatter | solution.py:17
  385.9 3.3 fusion.6
  389.2 0.0 all-gather.4.cloned.1.call-start
  389.2 183.1 %reduce-scatter.4.cloned.1.call-done = bf16[2,16,8192]{2,1,0:T(8,128)(2,1)} async-done(((bf16[2,512,8192]{2,1,0:T(8,128)(2,1)}), bf16[2,16,8192]{2,1,0:T(8,128)(2,1)}) %reduce-scatter.4.cloned.1.call-update) | async-done | bytes 524304 | tf_op jit(solution)/shard_map/reduce_scatter | solution.py:17
  572.3 3.6 fusion.2
  576.0 111.8 %all-gather.8.cloned.1.call-done = bf16[2,8192,512]{2,1,0:T(8,128)(2,1)} async-done(((bf16[2,256,512]{2,1,0:T(8,128)(2,1)}), bf16[2,8192,512]{2,1,0:T(8,128)(2,1)}) %all-gather.8.cloned.1.call-update) | async-done | bytes 16777232 | tf_op jit(solution)/shard_map/all_gather | solution.py:21
  687.7 116.0 %all-gather.6.cloned.1.call-done = bf16[2,512,8192]{2,1,0:T(8,128)(2,1)} async-done(((bf16[2,16,8192]{2,1,0:T(8,128)(2,1)}), bf16[2,512,8192]{2,1,0:T(8,128)(2,1)}) %all-gather.6.cloned.1.call-update) | async-done | bytes 16777232 | tf_op jit(solution)/shard_map/all_gather | solution.py:21
  803.7 116.0 %all-gather.4.cloned.1.call-done = bf16[2,512,8192]{2,1,0:T(8,128)(2,1)} async-done(((bf16[2,16,8192]{2,1,0:T(8,128)(2,1)}), bf16[2,512,8192]{2,1,0:T(8,128)(2,1)}) %all-gather.4.cloned.1.call-update) | async-done | bytes 16777232 | tf_op jit(solution)/shard_map/all_gather | solution.py:21
  919.6 16.7 %copy.24 = bf16[2,512,8192]{2,1,0:T(8,128)(2,1)} copy(bf16[2,512,8192]{2,1,0:T(8,128)(2,1)} %all-gather.4.cloned.1.call-done) | data formatting | bytes 33554432
  936.3 8.5 copy.25
  944.8 1.3 slice-done.2
  946.1 1.4 slice-done.3
  947.5 6.2 copy.26
  (17 shorter events, 0.1 us)
Async XLA Ops:
  7.2 192.3 %reduce-scatter.8.cloned.1.call-start = ((), (), s32[]{:S(2)}) async-start(), calls=%async_computation.7 | async-start | bytes 17301504 | tf_op jit(solution)/shard_map/reduce_scatter | solution.py:17
  7.9 378.0 %reduce-scatter.6.cloned.1.call-start = ((), (), s32[]{:S(2)}) async-start(), calls=%async_computation.5 | async-start | bytes 17301504 | tf_op jit(solution)/shard_map/reduce_scatter | solution.py:17
  8.0 191.5 %copy-start.1 = (f32[2,256,512]{2,1,0:T(8,128)S(1)}, f32[2,256,512]{2,1,0:T(8,128)}, u32[]{:S(2)}) copy-start(f32[2,256,512]{2,1,0:T(8,128)} %param.23) | copy-start | bytes 3145732
  8.0 191.5 %copy-start.2 = (f32[2,256,512]{2,1,0:T(8,128)S(1)}, f32[2,256,512]{2,1,0:T(8,128)}, u32[]{:S(2)}) copy-start(f32[2,256,512]{2,1,0:T(8,128)} %param.20) | copy-start | bytes 3145732
  8.0 377.9 %copy-start.3 = (f32[2,16,8192]{2,1,0:T(8,128)S(1)}, f32[2,16,8192]{2,1,0:T(8,128)}, u32[]{:S(2)}) copy-start(f32[2,16,8192]{2,1,0:T(8,128)} %param.22) | copy-start | bytes 3145732
  8.7 563.7 %reduce-scatter.4.cloned.1.call-start = ((), (), s32[]{:S(2)}) async-start(), calls=%async_computation.3 | async-start | bytes 17301504 | tf_op jit(solution)/shard_map/reduce_scatter | solution.py:17
  9.4 678.3 %all-gather.8.cloned.1.call-start = ((), (), s32[]{:S(2)}) async-start(), calls=%async_computation.8 | async-start | bytes 17301504 | tf_op jit(solution)/shard_map/all_gather | solution.py:21
  202.5 601.2 %all-gather.6.cloned.1.call-start = ((), (), s32[]{:S(2)}) async-start(), calls=%async_computation.6 | async-start | bytes 17301504 | tf_op jit(solution)/shard_map/all_gather | solution.py:21
  389.2 530.4 %all-gather.4.cloned.1.call-start = ((), (), s32[]{:S(2)}) async-start(), calls=%async_computation.4 | async-start | bytes 17301504 | tf_op jit(solution)/shard_map/all_gather | solution.py:21
  919.6 16.7 %copy-start = (bf16[2,512,8192]{2,1,0:T(8,128)(2,1)S(1)}, bf16[2,512,8192]{2,1,0:T(8,128)(2,1)}, u32[]{:S(2)}) copy-start(bf16[2,512,8192]{2,1,0:T(8,128)(2,1)} %all-gather.6.cloned.1.call-done) | copy-start | bytes 50331652
  919.6 25.2 %slice-start = ((s8[16777216]{0:T(1024)(128)(4,1)}), s8[4194304]{0:T(1024)(128)(4,1)S(1)}, s32[]{:S(2)}) async-start(s8[16777216]{0:T(1024)(128)(4,1)} %bitcast.6), calls=%async_computation.9 | async-start | bytes 8388608
  919.6 25.2 %slice-start.1 = ((s8[16777216]{0:T(1024)(128)(4,1)}), s8[4194304]{0:T(1024)(128)(4,1)S(1)}, s32[]{:S(2)}) async-start(s8[16777216]{0:T(1024)(128)(4,1)} %bitcast.6), calls=%async_computation.10 | async-start | bytes 8388608
  919.6 26.5 %slice-start.2 = ((s8[16777216]{0:T(1024)(128)(4,1)}), s8[4194304]{0:T(1024)(128)(4,1)S(1)}, s32[]{:S(2)}) async-start(s8[16777216]{0:T(1024)(128)(4,1)} %bitcast.6), calls=%async_computation.11 | async-start | bytes 8388608
  936.3 11.2 %slice-start.3 = ((s8[16777216]{0:T(1024)(128)(4,1)}), s8[4194304]{0:T(1024)(128)(4,1)S(1)}, s32[]{:S(2)}) async-start(s8[16777216]{0:T(1024)(128)(4,1)} %bitcast.6), calls=%async_computation.12 | async-start | bytes 8388608
Sparse Core Ops, SparseCore 0:
  10.3 189.1 reduce-scatter.7
  201.7 184.1 reduce-scatter.5
  388.2 184.1 reduce-scatter.3
  575.8 111.8 all-gather.7
  691.2 112.4 all-gather.5
  807.2 112.4 all-gather.3
where the time goes:
time: 961 us
  waiting for transfers between devices  902 us (94%)
  local copies, waits for them, and re-layouts  34.1 us (4%)
  between operations  14.2 us (1%)
  other arithmetic  9.87 us (1%)
    reduce_scatter x3, waiting for transfers between devices, step(): lax.psum_scatter(t[0], 'dp', scatter_dimension=1, tiled=True)  556 us
    all_gather x3, waiting for transfers between devices, step(): whole = [lax.all_gather(one[0], 'dp', axis=1, tiled=True) for one in new]  344 us
    unnamed x19, local copies, waits for them, and re-layouts  34.1 us
  transfers between devices with their start and end apart: 6, of which 6 were waited for; matrix products, arithmetic and copies ran while one was open for 1% of the time, Pallas kernels for 0%

commit v1 on v0

v1 whole, which is shorter than its diff:
```python
import functools

import jax
import jax.numpy as jnp
from jax import lax
from jax.experimental import pallas as pl
from jax.experimental.pallas import tpu as pltpu
from jax.sharding import PartitionSpec as P

F32, BF16 = jnp.float32, jnp.bfloat16
UNIT = 512

UNITS = 2
PER_LAYER = 16 // UNITS
CHUNKS = 6 * PER_LAYER

S1 = 1
T = S1 + 2
LZ = 1
FIN = T + 3 * LZ
NEW = FIN + 1
GZ = NEW + 2
G1 = GZ + 3 * LZ
G0 = G1 + 2
END = G0 + 2

SLOTS = 32
EARLY = 16
OWN = 4
SUMS = 8


def kernel(*refs):
    g, w, m, v, out, m_out, v_out = (refs[i : i + 3] for i in range(0, 21, 3))
    own, core, first, zs, last, last_send, new, sums, kept, wb, mb, vb, mo, vo, local, recv, zrecv, grecv, sent, stored = refs[21:]

    rep, me = lax.axis_index("rep"), lax.axis_index("dp")
    c, z, y, x = lax.rem(me, 2), lax.rem(lax.div(me, 2), 4), lax.rem(lax.div(me, 8), 2), lax.div(me, 16)
    other = me + 1 - 2 * c
    xn, yn = me + 16 * (1 - 2 * x), me + 8 * (1 - 2 * y)

    def order(k):
        odd = lax.rem(k, 2)
        pn, qn = xn + odd * (yn - xn), yn + odd * (xn - yn)
        p, q = x + odd * (y - x), y + odd * (x - y)
        return pn, qn, p, q, 8 - 4 * odd, 4 + 4 * odd

    def by_weight(k, body):
        at = lax.div(k, PER_LAYER)
        which, layer, piece = lax.div(at, 2), lax.rem(at, 2), lax.rem(k, PER_LAYER)
        for i in range(3):
            pl.when(which == i)(functools.partial(body, i, layer, piece))

    def cut(i, piece, u=None):
        start, n = (piece * UNITS, UNITS) if u is None else (piece * UNITS + u, 1)
        if i < 2:
            return slice(None), pl.ds(pl.multiple_of(start * UNIT, UNIT), n * UNIT)
        return pl.ds(pl.multiple_of(start * 16, 16), n * 16), slice(None)

    def send(src, dst, s, r, to):
        pltpu.make_async_remote_copy(src, dst, s, r, device_id=(rep, to), device_id_type=pl.DeviceIdType.MESH).start()

    def wait(like, sem):
        pltpu.make_async_copy(like, like, sem).wait()

    def stage(t, offset, body):
        k = t - offset
        pl.when(jnp.logical_and(k >= 0, k < CHUNKS))(functools.partial(body, k))

    CORE, FIRST, LAST, NEXT, GATHER1, GATHER0, GATHERZ = range(7)

    def start(k):
        s, e, o = lax.rem(k, SLOTS), lax.rem(k, EARLY), lax.rem(k, OWN)

        def body(i, layer, piece):
            for u in range(UNITS):
                rows, cols = cut(i, piece, u)
                send(g[i].at[layer, :, 1 - c, rows, cols], core.at[e, :, u], sent.at[CORE, s], recv.at[CORE, s], other)
                pltpu.make_async_copy(g[i].at[layer, :, c, rows, cols], own.at[o, :, u], local.at[o]).start()

        by_weight(k, body)

    def first_axis(k):
        s, e, o = lax.rem(k, SLOTS), lax.rem(k, EARLY), lax.rem(k, OWN)
        pn, _, p, _, sp, sq = order(k)
        wait(core.at[e], recv.at[CORE, s])
        wait(own.at[o], local.at[o])
        for q in range(2):
            j = (1 - p) * sp + q * sq

            @pl.loop(0, 4)
            def _(n):
                core[e, j + n] = (own[o, j + n].astype(F32) + core[e, j + n].astype(F32)).astype(BF16)

            send(core.at[e, pl.ds(j, 4)], first.at[e, q], sent.at[FIRST, s], recv.at[FIRST, s], pn)

    def sum_first(k):
        s, e, o, b = lax.rem(k, SLOTS), lax.rem(k, EARLY), lax.rem(k, OWN), lax.rem(k, SUMS)
        _, _, p, _, sp, sq = order(k)
        wait(first.at[e], recv.at[FIRST, s])
        for q in range(2):
            j = p * sp + q * sq

            @pl.loop(0, 4)
            def _(n):
                sums[b, n, q] = own[o, j + n].astype(F32) + core[e, j + n].astype(F32) + first[e, q, n].astype(F32)

    def hop(k, up):
        s, b = lax.rem(k, SLOTS), lax.rem(k, SUMS)
        for to in (3, 2, 1) if up else (0, 1, 2):
            slot = to + 1 if up else to

            @pl.when(to > z if up else to < z)
            def _():
                @pl.when(z > 0 if up else z < 3)
                def _():
                    wait(zs.at[s, slot], zrecv.at[s, slot])
                    for q in range(2):
                        zs[s, slot, q] = (sums[b, to, q] + zs[s, slot, q].astype(F32)).astype(BF16)

                @pl.when(z == 0 if up else z == 3)
                def _():
                    for q in range(2):
                        zs[s, slot, q] = sums[b, to, q].astype(BF16)

                send(zs.at[s, slot], zs.at[s, slot], sent.at[GATHERZ + 1, s], zrecv.at[s, slot], me + 2 if up else me - 2)

    def finish(k):
        s, b, h = lax.rem(k, SLOTS), lax.rem(k, SUMS), lax.rem(k, 2)
        _, qn, _, q, _, _ = order(k)

        @pl.when(z > 0)
        def _():
            wait(zs.at[s, z + 1], zrecv.at[s, z + 1])

        @pl.when(z < 3)
        def _():
            wait(zs.at[s, z], zrecv.at[s, z])

        def total(at):
            return sums[b, z, at]

        @pl.when(z == 0)
        def _():
            last_send[s] = (sums[b, z, 1 - q] + zs[s, z, 1 - q].astype(F32)).astype(BF16)
            kept[h] = sums[b, z, q] + zs[s, z, q].astype(F32)

        @pl.when(z == 3)
        def _():
            last_send[s] = (sums[b, z, 1 - q] + zs[s, z + 1, 1 - q].astype(F32)).astype(BF16)
            kept[h] = sums[b, z, q] + zs[s, z + 1, q].astype(F32)

        @pl.when(jnp.logical_and(z > 0, z < 3))
        def _():
            last_send[s] = (sums[b, z, 1 - q] + zs[s, z, 1 - q].astype(F32) + zs[s, z + 1, 1 - q].astype(F32)).astype(BF16)
            kept[h] = sums[b, z, q] + zs[s, z, q].astype(F32) + zs[s, z + 1, q].astype(F32)

        send(last_send.at[s], last.at[s], sent.at[LAST, s], recv.at[LAST, s], qn)

        def load(i, layer, piece):
            for u in range(UNITS):
                rows, cols = cut(i, piece, u)
                pltpu.make_async_copy(w[i].at[layer, me, rows, cols], wb.at[h, u], local.at[OWN + h]).start()
                pltpu.make_async_copy(m[i].at[layer, rows, cols], mb.at[h, u], local.at[OWN + 2 + h]).start()
                pltpu.make_async_copy(v[i].at[layer, rows, cols], vb.at[h, u], local.at[OWN + 4 + h]).start()

        by_weight(k, load)

    def wait_stored(h):
        wait(mo.at[h], stored.at[h])
        wait(vo.at[h], stored.at[2 + h])

    def update(k):
        s, h = lax.rem(k, SLOTS), lax.rem(k, 2)
        _, qn, _, _, _, _ = order(k)
        wait(last.at[s], recv.at[LAST, s])
        wait(wb.at[h], local.at[OWN + h])
        wait(mb.at[h], local.at[OWN + 2 + h])
        wait(vb.at[h], local.at[OWN + 4 + h])
        pl.when(k >= 2)(functools.partial(wait_stored, h))
        grad = (kept[h] + last[s].astype(F32)).astype(BF16).astype(F32)
        old = wb[h].astype(F32)
        mm = 0.9 * mb[h] + 0.1 * grad
        vv = 0.95 * vb[h] + 0.05 * grad * grad
        mo[h] = mm
        vo[h] = vv
        new[s] = (old - 0.02 * (mm * lax.rsqrt(vv + 1e-8) + 0.1 * old)).astype(BF16)

        def store(i, layer, piece):
            for u in range(UNITS):
                rows, cols = cut(i, piece, u)
                here = out[i].at[layer, lax.div(me, 2), c, rows, cols]
                send(new.at[s, u], here, sent.at[NEXT, s], recv.at[NEXT, s], qn)
                pltpu.make_async_copy(new.at[s, u], here, stored.at[4 + lax.rem(k, 4)]).start()
                pltpu.make_async_copy(mo.at[h, u], m_out[i].at[layer, rows, cols], stored.at[h]).start()
                pltpu.make_async_copy(vo.at[h, u], v_out[i].at[layer, rows, cols], stored.at[2 + h]).start()

        by_weight(k, store)

    def like(pieces):
        if pieces == 1:
            return out[0].at[0, 0, 0, :, pl.ds(0, UNITS * UNIT)]
        if pieces <= 16:
            return out[0].at[0, pl.ds(0, pieces), 0, :, pl.ds(0, UNITS * UNIT)]
        raise ValueError(pieces)

    def pass_on(k, at, up, down):
        s = lax.rem(k, SLOTS)
        _, _, p, _, sp, sq = order(k)

        def body(i, layer, piece):
            rows, cols = cut(i, piece)
            for cond, to in ((up, me + 2), (down, me - 2)):
                if cond is not None:

                    @pl.when(cond)
                    def _():
                        for q in range(2):
                            block = out[i].at[layer, p * sp + q * sq + at, c, rows, cols]
                            send(block, block, sent.at[GATHERZ, s], grecv.at[s, at], to)

        by_weight(k, body)

    def gather_own(k):
        s = lax.rem(k, SLOTS)
        wait(new.at[s], stored.at[4 + lax.rem(k, 4)])
        wait(new.at[s], recv.at[NEXT, s])
        pass_on(k, z, z < 3, z > 0)

    def gather_z(k, d):
        s = lax.rem(k, SLOTS)

        @pl.when(z - d >= 0)
        def _():
            wait(like(2), grecv.at[s, z - d])
            if d < 3:
                pass_on(k, z - d, z < 3, None)

        @pl.when(z + d <= 3)
        def _():
            wait(like(2), grecv.at[s, z + d])
            if d < 3:
                pass_on(k, z + d, None, z > 0)

    def gather_first(k):
        s = lax.rem(k, SLOTS)
        pn, _, p, _, sp, sq = order(k)

        def body(i, layer, piece):
            rows, cols = cut(i, piece)
            for q in range(2):
                block = out[i].at[layer, pl.ds(p * sp + q * sq, 4), c, rows, cols]
                send(block, block, sent.at[GATHER1, s], recv.at[GATHER1, s], pn)

        by_weight(k, body)

    def gather_core(k):
        s = lax.rem(k, SLOTS)
        wait(like(8), recv.at[GATHER1, s])

        def body(i, layer, piece):
            rows, cols = cut(i, piece)
            block = out[i].at[layer, :, c, rows, cols]
            send(block, block, sent.at[GATHER0, s], recv.at[GATHER0, s], other)

        by_weight(k, body)

    def sent_first(k):
        s, e = lax.rem(k, SLOTS), lax.rem(k, EARLY)
        wait(core.at[e], sent.at[CORE, s])
        wait(first.at[e], sent.at[FIRST, s])

    def end(k):
        s = lax.rem(k, SLOTS)
        wait(like(16), recv.at[GATHER0, s])
        wait(zs.at[s, pl.ds(0, 3)], sent.at[GATHERZ + 1, s])
        wait(last.at[s], sent.at[LAST, s])
        wait(new.at[s], sent.at[NEXT, s])
        pl.when(jnp.logical_or(z == 0, z == 3))(lambda: wait(like(2), sent.at[GATHERZ, s]))
        pl.when(jnp.logical_and(z > 0, z < 3))(lambda: wait(like(10), sent.at[GATHERZ, s]))
        wait(like(8), sent.at[GATHER1, s])
        wait(like(16), sent.at[GATHER0, s])

    @pl.loop(0, CHUNKS + END)
    def _(t):
        stage(t, END, end)
        stage(t, G0, gather_core)
        for d in (3, 2, 1):
            stage(t, GZ + d * LZ, functools.partial(gather_z, d=d))
        stage(t, G1, gather_first)
        stage(t, GZ, gather_own)
        stage(t, NEW, update)
        stage(t, T + 5, sent_first)
        stage(t, FIN, finish)
        stage(t, T, sum_first)
        stage(t, T + LZ * z, functools.partial(hop, up=True))
        stage(t, T + LZ * (3 - z), functools.partial(hop, up=False))
        stage(t, S1, first_axis)
        stage(t, 0, start)

    for h in range(2):
        wait_stored(h)


def solution(mesh):
    n = (UNITS, 16, UNIT)

    def step(*arrays):
        g, w, m, v = (arrays[i : i + 3] for i in (0, 3, 6, 9))
        shapes = [one.shape for one in w]
        g = [one.reshape(2, 16, 2, one.shape[2] // 32, one.shape[3]) for one in g]
        w = [one.reshape(2, 32, one.shape[1] // 32, one.shape[2]) for one in w]
        results = pl.pallas_call(
            kernel,
            name="step",
            in_specs=[pl.BlockSpec(memory_space=pl.ANY)] * 12,
            out_specs=[pl.BlockSpec(memory_space=pl.ANY)] * 9,
            out_shape=[jax.ShapeDtypeStruct(one.shape, BF16) for one in g] + [jax.ShapeDtypeStruct(one.shape, F32) for one in (*m, *v)],
            scratch_shapes=[
                pltpu.VMEM((OWN, 16, *n), BF16),
                pltpu.VMEM((EARLY, 16, *n), BF16),
                pltpu.VMEM((EARLY, 2, 4, *n), BF16),
                pltpu.VMEM((SLOTS, 5, 2, *n), BF16),
                pltpu.VMEM((SLOTS, *n), BF16),
                pltpu.VMEM((SLOTS, *n), BF16),
                pltpu.VMEM((SLOTS, *n), BF16),
                pltpu.VMEM((SUMS, 4, 2, *n), F32),
                pltpu.VMEM((2, *n), F32),
                pltpu.VMEM((2, *n), BF16),
                pltpu.VMEM((2, *n), F32),
                pltpu.VMEM((2, *n), F32),
                pltpu.VMEM((2, *n), F32),
                pltpu.VMEM((2, *n), F32),
                pltpu.SemaphoreType.DMA((OWN + 6,)),
                pltpu.SemaphoreType.DMA((6, SLOTS)),
                pltpu.SemaphoreType.DMA((SLOTS, 5)),
                pltpu.SemaphoreType.DMA((SLOTS, 4)),
                pltpu.SemaphoreType.DMA((8, SLOTS)),
                pltpu.SemaphoreType.DMA((8,)),
            ],
            compiler_params=pltpu.CompilerParams(has_side_effects=True, vmem_limit_bytes=67_043_328),
        )(*g, *w, *m, *v)
        return (*(one.reshape(shape) for one, shape in zip(results[:3], shapes, strict=True)), *results[3:])

    all_of, cut = P(None, None, None), P(None, "dp", None)
    return jax.shard_map(
        step,
        mesh=mesh,
        in_specs=(P(("rep", "dp"), None, None, None),) * 3 + (all_of,) * 3 + (cut,) * 6,
        out_specs=(P("rep", None, None),) * 3 + (P("rep", "dp", None),) * 6,
        check_vma=False,
    )
```

time: 961 us -> 397 us (0.41)
  waiting for transfers between devices: 902 us -> 0 us
  Pallas kernels: 0 us -> 354 us
  between operations: 14.2 us -> 0.71 us
  other arithmetic: 9.87 us -> 0.01 us
    reduce_scatter x3 -> x0, waiting for transfers between devices: 556 us -> none  [step(): lax.psum_scatter(t[0], 'dp', scatter_dimension=1, tiled=True)]
    pallas_call x0 -> x1, Pallas kernels: none -> 354 us  [step(): pl.pallas_call(kernel, name='step', in_specs=[pl.BlockSpec(memory_space=p...]
    all_gather x3 -> x0, waiting for transfers between devices: 344 us -> none  [step(): whole = [lax.all_gather(one[0], 'dp', axis=1, tiled=True) for one in new]]
    convert_element_type x3 -> x0, other arithmetic: 9.87 us -> none  [adamw(): return ((w - 0.02 * step).astype(jnp.bfloat16), m, v)]
    unnamed x19 -> x31, local copies, waits for them, and re-layouts: 34.1 us -> 41.5 us
  transfers between devices with their start and end apart: 6 -> 0, of which waited for: 6 -> 0; matrix products, arithmetic and copies ran while one was open for 1% -> 0% of each run, Pallas kernels for 0% -> 0%
where the time goes in v1:
time: 397 us; the launch traced here: 396 us
  Pallas kernels  354 us (89%)
  local copies, waits for them, and re-layouts  41.5 us (10%)
    pallas_call x1, Pallas kernels, step(): pl.pallas_call(kernel, name='step', in_specs=[pl.BlockSpec(memory_space=p...  354 us
    unnamed x31, local copies, waits for them, and re-layouts  41.5 us

profile of v1, /device:TPU:0, one launch (start us, length us, event | category | flops | bytes accessed | tf_op | source)
XLA Modules:
  0.0 396.4 jit_solution(3993212656043571572)
XLA Ops:
  0.6 354.2 %step.1 = (bf16[2,16,2,16,8192]{4,3,2,1,0:T(8,128)(2,1)}, bf16[2,16,2,16,8192]{4,3,2,1,0:T(8,128)(2,1)}, bf16[2,16,2,256,512]{4,3,2,1,0:T(8,128)(2,1)}, f32[2,16...) custom-call(bf16[2,16,2,16,8192]{4,3,2,1,0:T(8,128)(2,1)} %bitcast.9, ...), custom_call_target="tpu_custom_call" | custom-call | tf_op jit(solution)/shard_map/step/pallas_call | solution.py:313
  354.8 0.0 copy-start
  354.8 0.0 slice-start
  354.8 0.0 slice-start.1
  354.9 16.7 %copy.30 = bf16[2,512,8192]{2,1,0:T(8,128)(2,1)} copy(bf16[2,512,8192]{2,1,0:T(8,128)(2,1)} %bitcast.19) | data formatting | bytes 33554432
  371.5 0.0 copy-done
  371.6 8.5 %copy.31 = bf16[2,512,8192]{2,1,0:T(8,128)(2,1)} copy(bf16[2,512,8192]{2,1,0:T(8,128)(2,1)S(1)} %bitcast.18) | data formatting | bytes 33554432
  380.1 0.0 slice-done
  380.1 0.0 slice-done.1
  380.1 1.5 slice-done.2
  381.5 1.2 slice-done.3
  382.8 0.0 copy-start.2
  382.8 0.0 copy-start.1
  382.8 7.8 %copy.32 = bf16[2,8192,512]{2,1,0:T(8,128)(2,1)} copy(bf16[2,8192,512]{2,1,0:T(8,128)(2,1)S(1)} %bitcast.17) | data formatting | bytes 33554432
  390.5 0.0 copy-done.6
  390.5 1.0 copy.33
  391.5 0.0 copy-done.5
  391.5 1.0 copy.34
  392.5 0.0 copy-done.4
  392.5 1.0 copy.35
  393.5 1.0 copy.36
  394.4 1.0 copy.37
  395.4 0.0 copy-done.1
  395.4 1.0 copy.38
  (9 shorter events, 0.0 us)
Async XLA Ops:
  354.8 16.7 %copy-start = (bf16[2,16,2,16,8192]{4,3,2,1,0:T(8,128)(2,1)S(1)}, bf16[2,16,2,16,8192]{4,3,2,1,0:T(8,128)(2,1)}, u32[]{:S(2)}) copy-start(bf16[2,16,2,16,8192]{4,3,2,1,0:T(8,128)(2,1)} %get-tuple-element.19) | copy-start | bytes 50331652
  354.8 25.2 %slice-start = ((s8[16777216]{0:T(1024)(128)(4,1)}), s8[4194304]{0:T(1024)(128)(4,1)S(1)}, s32[]{:S(2)}) async-start(s8[16777216]{0:T(1024)(128)(4,1)} %bitcast.15), calls=%async_computation | async-start | bytes 8388608
  354.8 25.2 %slice-start.1 = ((s8[16777216]{0:T(1024)(128)(4,1)}), s8[4194304]{0:T(1024)(128)(4,1)S(1)}, s32[]{:S(2)}) async-start(s8[16777216]{0:T(1024)(128)(4,1)} %bitcast.15), calls=%async_computation.1 | async-start | bytes 8388608
  371.5 10.0 %slice-start.2 = ((s8[16777216]{0:T(1024)(128)(4,1)}), s8[4194304]{0:T(1024)(128)(4,1)S(1)}, s32[]{:S(2)}) async-start(s8[16777216]{0:T(1024)(128)(4,1)} %bitcast.15), calls=%async_computation.2 | async-start | bytes 8388608
  371.6 11.2 %slice-start.3 = ((s8[16777216]{0:T(1024)(128)(4,1)}), s8[4194304]{0:T(1024)(128)(4,1)S(1)}, s32[]{:S(2)}) async-start(s8[16777216]{0:T(1024)(128)(4,1)} %bitcast.15), calls=%async_computation.3 | async-start | bytes 8388608
  382.7 7.8 %copy-start.6 = (f32[2,16,8192]{2,1,0:T(8,128)S(1)}, f32[2,16,8192]{2,1,0:T(8,128)}, u32[]{:S(2)}) copy-start(f32[2,16,8192]{2,1,0:T(8,128)} %get-tuple-element.39) | copy-start | bytes 3145732
  382.7 8.8 %copy-start.5 = (f32[2,16,8192]{2,1,0:T(8,128)S(1)}, f32[2,16,8192]{2,1,0:T(8,128)}, u32[]{:S(2)}) copy-start(f32[2,16,8192]{2,1,0:T(8,128)} %get-tuple-element.40) | copy-start | bytes 3145732
  382.7 9.7 %copy-start.4 = (f32[2,256,512]{2,1,0:T(8,128)S(1)}, f32[2,256,512]{2,1,0:T(8,128)}, u32[]{:S(2)}) copy-start(f32[2,256,512]{2,1,0:T(8,128)} %get-tuple-element.41) | copy-start | bytes 3145732
  382.7 10.7 %copy-start.3 = (f32[2,16,8192]{2,1,0:T(8,128)S(1)}, f32[2,16,8192]{2,1,0:T(8,128)}, u32[]{:S(2)}) copy-start(f32[2,16,8192]{2,1,0:T(8,128)} %get-tuple-element.42) | copy-start | bytes 3145732
  382.8 11.7 %copy-start.2 = (f32[2,16,8192]{2,1,0:T(8,128)S(1)}, f32[2,16,8192]{2,1,0:T(8,128)}, u32[]{:S(2)}) copy-start(f32[2,16,8192]{2,1,0:T(8,128)} %get-tuple-element.43) | copy-start | bytes 3145732
  382.8 12.6 %copy-start.1 = (f32[2,256,512]{2,1,0:T(8,128)S(1)}, f32[2,256,512]{2,1,0:T(8,128)}, u32[]{:S(2)}) copy-start(f32[2,256,512]{2,1,0:T(8,128)} %get-tuple-element.44) | copy-start | bytes 3145732

commit v2 on v1

--- a/solution.py
+++ b/solution.py
@@ -13,26 +13,25 @@
 UNITS = 2
 PER_LAYER = 16 // UNITS
 CHUNKS = 6 * PER_LAYER
+IN_VMEM = 2
 
 S1 = 1
 T = S1 + 2
 LZ = 1
 FIN = T + 3 * LZ
 NEW = FIN + 1
-GZ = NEW + 2
+GZ = NEW + 1
 G1 = GZ + 3 * LZ
 G0 = G1 + 2
 END = G0 + 2
 
 SLOTS = 32
-EARLY = 16
-OWN = 4
-SUMS = 8
+OWN, CORE_SLOTS, FIRST_SLOTS, Z_SLOTS, LAST_SLOTS, SUMS = 4, 6, 4, 8, 8, 4
 
 
 def kernel(*refs):
     g, w, m, v, out, m_out, v_out = (refs[i : i + 3] for i in range(0, 21, 3))
-    own, core, first, zs, last, last_send, new, sums, kept, wb, mb, vb, mo, vo, local, recv, zrecv, grecv, sent, stored = refs[21:]
+    own, core, first, zs, last, last_send, fresh, sums, kept, wb, mb, vb, mo, vo, local, recv, zrecv, grecv, sent, stored = refs[21:]
 
     rep, me = lax.axis_index("rep"), lax.axis_index("dp")
     c, z, y, x = lax.rem(me, 2), lax.rem(lax.div(me, 2), 4), lax.rem(lax.div(me, 8), 2), lax.div(me, 16)
@@ -70,7 +69,7 @@
     CORE, FIRST, LAST, NEXT, GATHER1, GATHER0, GATHERZ = range(7)
 
     def start(k):
-        s, e, o = lax.rem(k, SLOTS), lax.rem(k, EARLY), lax.rem(k, OWN)
+        s, e, o = lax.rem(k, SLOTS), lax.rem(k, CORE_SLOTS), lax.rem(k, OWN)
 
         def body(i, layer, piece):
             for u in range(UNITS):
@@ -81,7 +80,7 @@
         by_weight(k, body)
 
     def first_axis(k):
-        s, e, o = lax.rem(k, SLOTS), lax.rem(k, EARLY), lax.rem(k, OWN)
+        s, e, f, o = lax.rem(k, SLOTS), lax.rem(k, CORE_SLOTS), lax.rem(k, FIRST_SLOTS), lax.rem(k, OWN)
         pn, _, p, _, sp, sq = order(k)
         wait(core.at[e], recv.at[CORE, s])
         wait(own.at[o], local.at[o])
@@ -92,21 +91,21 @@
             def _(n):
                 core[e, j + n] = (own[o, j + n].astype(F32) + core[e, j + n].astype(F32)).astype(BF16)
 
-            send(core.at[e, pl.ds(j, 4)], first.at[e, q], sent.at[FIRST, s], recv.at[FIRST, s], pn)
+            send(core.at[e, pl.ds(j, 4)], first.at[f, q], sent.at[FIRST, s], recv.at[FIRST, s], pn)
 
     def sum_first(k):
-        s, e, o, b = lax.rem(k, SLOTS), lax.rem(k, EARLY), lax.rem(k, OWN), lax.rem(k, SUMS)
+        s, e, f, o, b = lax.rem(k, SLOTS), lax.rem(k, CORE_SLOTS), lax.rem(k, FIRST_SLOTS), lax.rem(k, OWN), lax.rem(k, SUMS)
         _, _, p, _, sp, sq = order(k)
-        wait(first.at[e], recv.at[FIRST, s])
+        wait(first.at[f], recv.at[FIRST, s])
         for q in range(2):
             j = p * sp + q * sq
 
             @pl.loop(0, 4)
             def _(n):
-                sums[b, n, q] = own[o, j + n].astype(F32) + core[e, j + n].astype(F32) + first[e, q, n].astype(F32)
+                sums[b, n, q] = own[o, j + n].astype(F32) + core[e, j + n].astype(F32) + first[f, q, n].astype(F32)
 
     def hop(k, up):
-        s, b = lax.rem(k, SLOTS), lax.rem(k, SUMS)
+        s, n, b = lax.rem(k, SLOTS), lax.rem(k, Z_SLOTS), lax.rem(k, SUMS)
         for to in (3, 2, 1) if up else (0, 1, 2):
             slot = to + 1 if up else to
 
@@ -114,48 +113,45 @@
             def _():
                 @pl.when(z > 0 if up else z < 3)
                 def _():
-                    wait(zs.at[s, slot], zrecv.at[s, slot])
+                    wait(zs.at[n, slot], zrecv.at[s, slot])
                     for q in range(2):
-                        zs[s, slot, q] = (sums[b, to, q] + zs[s, slot, q].astype(F32)).astype(BF16)
+                        zs[n, slot, q] = (sums[b, to, q] + zs[n, slot, q].astype(F32)).astype(BF16)
 
                 @pl.when(z == 0 if up else z == 3)
                 def _():
                     for q in range(2):
-                        zs[s, slot, q] = sums[b, to, q].astype(BF16)
-
-                send(zs.at[s, slot], zs.at[s, slot], sent.at[GATHERZ + 1, s], zrecv.at[s, slot], me + 2 if up else me - 2)
+                        zs[n, slot, q] = sums[b, to, q].astype(BF16)
+
+                send(zs.at[n, slot], zs.at[n, slot], sent.at[GATHERZ + 1, s], zrecv.at[s, slot], me + 2 if up else me - 2)
 
     def finish(k):
-        s, b, h = lax.rem(k, SLOTS), lax.rem(k, SUMS), lax.rem(k, 2)
+        s, n, r, b, h = lax.rem(k, SLOTS), lax.rem(k, Z_SLOTS), lax.rem(k, LAST_SLOTS), lax.rem(k, SUMS), lax.rem(k, 2)
         _, qn, _, q, _, _ = order(k)
 
         @pl.when(z > 0)
         def _():
-            wait(zs.at[s, z + 1], zrecv.at[s, z + 1])
+            wait(zs.at[n, z + 1], zrecv.at[s, z + 1])
 
         @pl.when(z < 3)
         def _():
-            wait(zs.at[s, z], zrecv.at[s, z])
-
-        def total(at):
-            return sums[b, z, at]
+            wait(zs.at[n, z], zrecv.at[s, z])
 
         @pl.when(z == 0)
         def _():
-            last_send[s] = (sums[b, z, 1 - q] + zs[s, z, 1 - q].astype(F32)).astype(BF16)
-            kept[h] = sums[b, z, q] + zs[s, z, q].astype(F32)
+            last_send[r] = (sums[b, z, 1 - q] + zs[n, z, 1 - q].astype(F32)).astype(BF16)
+            kept[h] = sums[b, z, q] + zs[n, z, q].astype(F32)
 
         @pl.when(z == 3)
         def _():
-            last_send[s] = (sums[b, z, 1 - q] + zs[s, z + 1, 1 - q].astype(F32)).astype(BF16)
-            kept[h] = sums[b, z, q] + zs[s, z + 1, q].astype(F32)
+            last_send[r] = (sums[b, z, 1 - q] + zs[n, z + 1, 1 - q].astype(F32)).astype(BF16)
+            kept[h] = sums[b, z, q] + zs[n, z + 1, q].astype(F32)
 
         @pl.when(jnp.logical_and(z > 0, z < 3))
         def _():
-            last_send[s] = (sums[b, z, 1 - q] + zs[s, z, 1 - q].astype(F32) + zs[s, z + 1, 1 - q].astype(F32)).astype(BF16)
-            kept[h] = sums[b, z, q] + zs[s, z, q].astype(F32) + zs[s, z + 1, q].astype(F32)
-
-        send(last_send.at[s], last.at[s], sent.at[LAST, s], recv.at[LAST, s], qn)
+            last_send[r] = (sums[b, z, 1 - q] + zs[n, z, 1 - q].astype(F32) + zs[n, z + 1, 1 - q].astype(F32)).astype(BF16)
+            kept[h] = sums[b, z, q] + zs[n, z, q].astype(F32) + zs[n, z + 1, q].astype(F32)
+
+        send(last_send.at[r], last.at[r], sent.at[LAST, s], recv.at[LAST, s], qn)
 
         def load(i, layer, piece):
             for u in range(UNITS):
@@ -171,29 +167,37 @@
         wait(vo.at[h], stored.at[2 + h])
 
     def update(k):
-        s, h = lax.rem(k, SLOTS), lax.rem(k, 2)
+        s, r, h = lax.rem(k, SLOTS), lax.rem(k, LAST_SLOTS), lax.rem(k, 2)
         _, qn, _, _, _, _ = order(k)
-        wait(last.at[s], recv.at[LAST, s])
+        wait(last.at[r], recv.at[LAST, s])
         wait(wb.at[h], local.at[OWN + h])
         wait(mb.at[h], local.at[OWN + 2 + h])
         wait(vb.at[h], local.at[OWN + 4 + h])
         pl.when(k >= 2)(functools.partial(wait_stored, h))
-        grad = (kept[h] + last[s].astype(F32)).astype(BF16).astype(F32)
+        grad = (kept[h] + last[r].astype(F32)).astype(BF16).astype(F32)
         old = wb[h].astype(F32)
         mm = 0.9 * mb[h] + 0.1 * grad
         vv = 0.95 * vb[h] + 0.05 * grad * grad
         mo[h] = mm
         vo[h] = vv
-        new[s] = (old - 0.02 * (mm * lax.rsqrt(vv + 1e-8) + 0.1 * old)).astype(BF16)
+        new = (old - 0.02 * (mm * lax.rsqrt(vv + 1e-8) + 0.1 * old)).astype(BF16)
 
         def store(i, layer, piece):
             for u in range(UNITS):
                 rows, cols = cut(i, piece, u)
-                here = out[i].at[layer, lax.div(me, 2), c, rows, cols]
-                send(new.at[s, u], here, sent.at[NEXT, s], recv.at[NEXT, s], qn)
-                pltpu.make_async_copy(new.at[s, u], here, stored.at[4 + lax.rem(k, 4)]).start()
                 pltpu.make_async_copy(mo.at[h, u], m_out[i].at[layer, rows, cols], stored.at[h]).start()
                 pltpu.make_async_copy(vo.at[h, u], v_out[i].at[layer, rows, cols], stored.at[2 + h]).start()
+                here = out[i].at[layer, lax.div(me, 2), c, rows, cols]
+                if i < IN_VMEM:
+                    here[...] = new[u]
+                else:
+                    fresh[r, u] = new[u]
+                    send(fresh.at[r, u], here, sent.at[NEXT, s], recv.at[NEXT, s], qn)
+                    pltpu.make_async_copy(fresh.at[r, u], here, stored.at[4 + r]).start()
+            if i < IN_VMEM:
+                rows, cols = cut(i, piece)
+                block = out[i].at[layer, lax.div(me, 2), c, rows, cols]
+                send(block, block, sent.at[NEXT, s], recv.at[NEXT, s], qn)
 
         by_weight(k, store)
 
@@ -223,8 +227,8 @@
 
     def gather_own(k):
         s = lax.rem(k, SLOTS)
-        wait(new.at[s], stored.at[4 + lax.rem(k, 4)])
-        wait(new.at[s], recv.at[NEXT, s])
+        wait(like(1), recv.at[NEXT, s])
+        pl.when(k >= IN_VMEM * 2 * PER_LAYER)(lambda: wait(fresh.at[0], stored.at[4 + lax.rem(k, LAST_SLOTS)]))
         pass_on(k, z, z < 3, z > 0)
 
     def gather_z(k, d):
@@ -266,16 +270,21 @@
         by_weight(k, body)
 
     def sent_first(k):
-        s, e = lax.rem(k, SLOTS), lax.rem(k, EARLY)
-        wait(core.at[e], sent.at[CORE, s])
-        wait(first.at[e], sent.at[FIRST, s])
+        s = lax.rem(k, SLOTS)
+        wait(core.at[0], sent.at[CORE, s])
+        wait(first.at[0], sent.at[FIRST, s])
+
+    def sent_new(k):
+        wait(like(1), sent.at[NEXT, lax.rem(k, SLOTS)])
+
+    def sent_sums(k):
+        s = lax.rem(k, SLOTS)
+        wait(zs.at[0, pl.ds(0, 3)], sent.at[GATHERZ + 1, s])
+        wait(last.at[0], sent.at[LAST, s])
 
     def end(k):
         s = lax.rem(k, SLOTS)
         wait(like(16), recv.at[GATHER0, s])
-        wait(zs.at[s, pl.ds(0, 3)], sent.at[GATHERZ + 1, s])
-        wait(last.at[s], sent.at[LAST, s])
-        wait(new.at[s], sent.at[NEXT, s])
         pl.when(jnp.logical_or(z == 0, z == 3))(lambda: wait(like(2), sent.at[GATHERZ, s]))
         pl.when(jnp.logical_and(z > 0, z < 3))(lambda: wait(like(10), sent.at[GATHERZ, s]))
         wait(like(8), sent.at[GATHER1, s])
@@ -290,7 +299,9 @@
         stage(t, G1, gather_first)
         stage(t, GZ, gather_own)
         stage(t, NEW, update)
-        stage(t, T + 5, sent_first)
+        stage(t, NEW + 6, sent_new)
+        stage(t, FIN + 3, sent_sums)
+        stage(t, T + 2, sent_first)
         stage(t, FIN, finish)
         stage(t, T, sum_first)
         stage(t, T + LZ * z, functools.partial(hop, up=True))
@@ -313,17 +324,17 @@
         results = pl.pallas_call(
             kernel,
             name="step",
-            in_specs=[pl.BlockSpec(memory_space=pl.ANY)] * 12,
-            out_specs=[pl.BlockSpec(memory_space=pl.ANY)] * 9,
-            out_shape=[jax.ShapeDtypeStruct(one.shape, BF16) for one in g] + [jax.ShapeDtypeStruct(one.shape, F32) for one in (*m, *v)],
+            in_specs=[pl.BlockSpec(memory_space=pltpu.HBM)] * 12,
+            out_specs=[pl.BlockSpec(memory_space=pltpu.VMEM)] * 2 + [pl.BlockSpec(memory_space=pltpu.HBM)] * 7,
+            out_shape=[pltpu.VMEM(one.shape, BF16) for one in g[:2]] + [jax.ShapeDtypeStruct(g[2].shape, BF16)] + [jax.ShapeDtypeStruct(one.shape, F32) for one in (*m, *v)],
             scratch_shapes=[
                 pltpu.VMEM((OWN, 16, *n), BF16),
-                pltpu.VMEM((EARLY, 16, *n), BF16),
-                pltpu.VMEM((EARLY, 2, 4, *n), BF16),
-                pltpu.VMEM((SLOTS, 5, 2, *n), BF16),
-                pltpu.VMEM((SLOTS, *n), BF16),
-                pltpu.VMEM((SLOTS, *n), BF16),
-                pltpu.VMEM((SLOTS, *n), BF16),
+                pltpu.VMEM((CORE_SLOTS, 16, *n), BF16),
+                pltpu.VMEM((FIRST_SLOTS, 2, 4, *n), BF16),
+                pltpu.VMEM((Z_SLOTS, 5, 2, *n), BF16),
+                pltpu.VMEM((LAST_SLOTS, *n), BF16),
+                pltpu.VMEM((LAST_SLOTS, *n), BF16),
+                pltpu.VMEM((LAST_SLOTS, *n), BF16),
                 pltpu.VMEM((SUMS, 4, 2, *n), F32),
                 pltpu.VMEM((2, *n), F32),
                 pltpu.VMEM((2, *n), BF16),
@@ -336,9 +347,9 @@
                 pltpu.SemaphoreType.DMA((SLOTS, 5)),
                 pltpu.SemaphoreType.DMA((SLOTS, 4)),
                 pltpu.SemaphoreType.DMA((8, SLOTS)),
-                pltpu.SemaphoreType.DMA((8,)),
+                pltpu.SemaphoreType.DMA((4 + LAST_SLOTS,)),
             ],
-            compiler_params=pltpu.CompilerParams(has_side_effects=True, vmem_limit_bytes=67_043_328),
+            compiler_params=pltpu.CompilerParams(has_side_effects=True, vmem_limit_bytes=16 * 2**20),
         )(*g, *w, *m, *v)
         return (*(one.reshape(shape) for one, shape in zip(results[:3], shapes, strict=True)), *results[3:])
 

time: 397 us -> 381 us (0.960)
  local copies, waits for them, and re-layouts: 41.5 us -> 30 us
  Pallas kernels: 354 us -> 350 us
    unnamed x31 -> x13, local copies, waits for them, and re-layouts: 41.5 us -> 30 us
    pallas_call x1, Pallas kernels: 354 us -> 350 us  [step(): pl.pallas_call(kernel, name='step', in_specs=[pl.BlockSpec(memory_space=p...]
where the time goes in v2:
time: 381 us
  Pallas kernels  350 us (92%)
  local copies, waits for them, and re-layouts  30 us (8%)
    pallas_call x1, Pallas kernels, step(): pl.pallas_call(kernel, name='step', in_specs=[pl.BlockSpec(memory_space=p...  350 us
    unnamed x13, local copies, waits for them, and re-layouts  30 us

profile of v2, /device:TPU:0, one launch (start us, length us, event | category | flops | bytes accessed | tf_op | source)
XLA Modules:
  0.0 380.6 jit_solution(8793065007505371201)
XLA Ops:
  0.6 350.0 %step.1 = (bf16[2,16,2,16,8192]{4,3,2,1,0:T(8,128)(2,1)S(1)}, bf16[2,16,2,16,8192]{4,3,2,1,0:T(8,128)(2,1)S(1)}, bf16[2,16,2,256,512]{4,3,2,1,0:T(8,128)(2,1)}, ...) custom-call(bf16[2,16,2,16,8192]{4,3,2,1,0:T(8,128)(2,1)} %bitcast.1, ...), custom_call_target="tpu_custom_call" | custom-call | tf_op jit(solution)/shard_map/step/pallas_call | solution.py:324
  350.6 6.2 %copy.30 = bf16[2,512,8192]{2,1,0:T(8,128)(2,1)} copy(bf16[2,512,8192]{2,1,0:T(8,128)(2,1)S(1)} %bitcast.10) | data formatting | bytes 33554432
  356.8 0.0 copy-start
  356.8 8.5 %copy.31 = bf16[2,512,8192]{2,1,0:T(8,128)(2,1)} copy(bf16[2,512,8192]{2,1,0:T(8,128)(2,1)S(1)} %bitcast.9) | data formatting | bytes 33554432
  365.3 3.3 copy-done
  368.6 0.0 copy-start.1
  368.6 6.2 %copy.32 = bf16[2,8192,512]{2,1,0:T(8,128)(2,1)} copy(bf16[2,8192,512]{2,1,0:T(8,128)(2,1)S(1)} %bitcast.17) | data formatting | bytes 33554432
  374.8 1.0 copy.33
  375.7 1.0 copy.34
  376.7 1.0 copy.35
  377.7 1.0 copy.36
  378.6 1.0 copy.37
  379.6 0.0 copy-done.1
  379.6 1.0 copy.38
Async XLA Ops:
  356.8 11.8 %copy-start = (bf16[2,16,2,256,512]{4,3,2,1,0:T(8,128)(2,1)S(1)}, bf16[2,16,2,256,512]{4,3,2,1,0:T(8,128)(2,1)}, u32[]{:S(2)}) copy-start(bf16[2,16,2,256,512]{4,3,2,1,0:T(8,128)(2,1)} %get-tuple-element.20) | copy-start | bytes 50331652
  368.6 11.0 %copy-start.1 = (f32[2,256,512]{2,1,0:T(8,128)S(1)}, f32[2,256,512]{2,1,0:T(8,128)}, u32[]{:S(2)}) copy-start(f32[2,256,512]{2,1,0:T(8,128)} %get-tuple-element.53) | copy-start | bytes 3145732

commit v3 on v0

v3 whole, which is shorter than its diff:
```python
import functools

import jax
import jax.numpy as jnp
from jax import lax
from jax.experimental import pallas as pl
from jax.experimental.pallas import tpu as pltpu
from jax.sharding import PartitionSpec as P

F32, BF16 = jnp.float32, jnp.bfloat16
UNIT = 512

UNITS = 1
PER_LAYER = 16 // UNITS
CHUNKS = 6 * PER_LAYER
VMEM_MIB = 16
IN_VMEM = 2

S1 = 2
T = S1 + 3
LZ = 2
FIN = T + 3 * LZ
NEW = FIN + 2
GZ = NEW + 2
G1 = GZ + 3 * LZ
G0 = G1 + 3
END = G0 + 2

SLOTS = 32
OWN, CORE_SLOTS, FIRST_SLOTS, Z_SLOTS, LAST_SLOTS, SUMS = 8, 16, 8, 16, 16, 8


def kernel(*refs):
    g, w, m, v, out, m_out, v_out = (refs[i : i + 3] for i in range(0, 21, 3))
    own, core, first, zs, last, last_send, fresh, sums, kept, *held = refs[21:33]
    whole, local, recv, zrecv, grecv, sent, stored = refs[33:]

    rep, me = lax.axis_index("rep"), lax.axis_index("dp")
    c, z, y, x = lax.rem(me, 2), lax.rem(lax.div(me, 2), 4), lax.rem(lax.div(me, 8), 2), lax.div(me, 16)
    other = me + 1 - 2 * c
    across = (me + 16 * (1 - 2 * x), me + 8 * (1 - 2 * y))

    def pair(odd, p, *rest):
        return (slice(None), p, *rest) if odd else (p, slice(None), *rest)

    def by_weight(k, body):
        at = lax.div(k, PER_LAYER)
        which, layer, piece = lax.div(at, 2), lax.rem(at, 2), lax.rem(k, PER_LAYER)
        for i in range(3):
            pl.when(which == i)(functools.partial(body, i, layer, piece))

    def cut(i, piece, u=None):
        start, n = (piece * UNITS, UNITS) if u is None else (piece * UNITS + u, 1)
        if i < 2:
            return slice(None), pl.ds(pl.multiple_of(start * UNIT, UNIT), n * UNIT)
        return pl.ds(pl.multiple_of(start * 16, 16), n * 16), slice(None)

    def send(src, dst, s, r, to):
        pltpu.make_async_remote_copy(src, dst, s, r, device_id=(rep, to), device_id_type=pl.DeviceIdType.MESH).start()

    def wait(like, sem):
        pltpu.make_async_copy(like, like, sem).wait()

    CORE, FIRST, LAST, NEXT, GATHER1, GATHER0, GATHERZ, SUMZ = range(8)
    every = slice(None)

    loads = [pltpu.make_async_copy(a, b, whole.at[i]) for i, (a, b) in enumerate(zip((*m, *v), (*m_out, *v_out), strict=True))]
    loads += [pltpu.make_async_copy(w[i].at[:, me], held[i], whole.at[6 + i]) for i in range(3)]

    def start(k, odd):
        s, e, o = lax.rem(k, SLOTS), lax.rem(k, CORE_SLOTS), lax.rem(k, OWN)

        def body(i, layer, piece):
            for u in range(UNITS):
                rows, cols = cut(i, piece, u)
                send(g[i].at[layer, :, :, :, 1 - c, rows, cols], core.at[e, :, :, :, u], sent.at[CORE, s], recv.at[CORE, s], other)
                pltpu.make_async_copy(g[i].at[layer, :, :, :, c, rows, cols], own.at[o, :, :, :, u], local.at[o]).start()

        by_weight(k, body)

    def first_axis(k, odd):
        s, e, f, o = lax.rem(k, SLOTS), lax.rem(k, CORE_SLOTS), lax.rem(k, FIRST_SLOTS), lax.rem(k, OWN)
        p = 1 - (y if odd else x)
        wait(core.at[e], recv.at[CORE, s])
        wait(own.at[o], local.at[o])

        @pl.loop(0, 4)
        def _(n):
            at = pair(odd, p, n)
            core[e, *at] = (own[o, *at].astype(F32) + core[e, *at].astype(F32)).astype(BF16)

        send(core.at[e, *pair(odd, p)], first.at[f], sent.at[FIRST, s], recv.at[FIRST, s], across[odd])

    def sum_first(k, odd):
        s, e, f, o, b = lax.rem(k, SLOTS), lax.rem(k, CORE_SLOTS), lax.rem(k, FIRST_SLOTS), lax.rem(k, OWN), lax.rem(k, SUMS)
        p = y if odd else x
        wait(first.at[f], recv.at[FIRST, s])

        @pl.loop(0, 4)
        def _(n):
            at = pair(odd, p, n)
            sums[b, n] = own[o, *at].astype(F32) + core[e, *at].astype(F32) + first[f, :, n].astype(F32)

    def hop(k, up):
        s, n, b = lax.rem(k, SLOTS), lax.rem(k, Z_SLOTS), lax.rem(k, SUMS)
        for to in (3, 2, 1) if up else (0, 1, 2):
            slot = to + 1 if up else to

            @pl.when(to > z if up else to < z)
            def _():
                @pl.when(z > 0 if up else z < 3)
                def _():
                    wait(zs.at[n, slot], zrecv.at[s, slot])
                    zs[n, slot] = (sums[b, to] + zs[n, slot].astype(F32)).astype(BF16)

                @pl.when(z == 0 if up else z == 3)
                def _():
                    zs[n, slot] = sums[b, to].astype(BF16)

                send(zs.at[n, slot], zs.at[n, slot], sent.at[SUMZ, s], zrecv.at[s, slot], me + 2 if up else me - 2)

    def finish(k, odd):
        s, n, r, b, h = lax.rem(k, SLOTS), lax.rem(k, Z_SLOTS), lax.rem(k, LAST_SLOTS), lax.rem(k, SUMS), lax.rem(k, 2)
        q = x if odd else y

        @pl.when(z > 0)
        def _():
            wait(zs.at[n, z + 1], zrecv.at[s, z + 1])

        @pl.when(z < 3)
        def _():
            wait(zs.at[n, z], zrecv.at[s, z])

        def put_total(*slots):
            for to in (1 - q, q):
                total = sums[b, z, to]
                for slot in slots:
                    total = total + zs[n, slot, to].astype(F32)
                if to is q:
                    kept[h] = total
                else:
                    last_send[r] = total.astype(BF16)

        pl.when(z == 0)(lambda: put_total(z))
        pl.when(z == 3)(lambda: put_total(z + 1))
        pl.when(jnp.logical_and(z > 0, z < 3))(lambda: put_total(z, z + 1))
        send(last_send.at[r], last.at[r], sent.at[LAST, s], recv.at[LAST, s], across[1 - odd])

    def update(k, odd):
        s, r, h = lax.rem(k, SLOTS), lax.rem(k, LAST_SLOTS), lax.rem(k, 2)

        @pl.when(k == 0)
        def _():
            for one in loads:
                one.wait()

        wait(last.at[r], recv.at[LAST, s])

        def store(i, layer, piece):
            for u in range(UNITS):
                rows, cols = cut(i, piece, u)
                grad = (kept[h, u] + last[r, u].astype(F32)).astype(BF16).astype(F32)
                old = held[i][layer, rows, cols].astype(F32)
                mm = 0.9 * m_out[i][layer, rows, cols] + 0.1 * grad
                vv = 0.95 * v_out[i][layer, rows, cols] + 0.05 * grad * grad
                m_out[i][layer, rows, cols] = mm
                v_out[i][layer, rows, cols] = vv
                new = (old - 0.02 * (mm * lax.rsqrt(vv + 1e-8) + 0.1 * old)).astype(BF16)
                here = out[i].at[layer, x, y, z, c, rows, cols]
                if i < IN_VMEM:
                    here[...] = new
                else:
                    fresh[r, u] = new
                    send(fresh.at[r, u], here, sent.at[NEXT, s], recv.at[NEXT, s], across[1 - odd])
                    pltpu.make_async_copy(fresh.at[r, u], here, stored.at[r]).start()
            if i < IN_VMEM:
                block = out[i].at[layer, x, y, z, c, *cut(i, piece)]
                send(block, block, sent.at[NEXT, s], recv.at[NEXT, s], across[1 - odd])

        by_weight(k, store)

    def like(pieces):
        if pieces == 1:
            return last.at[0]
        return zs.at[0] if pieces == 10 else zs.at[0, 0] if pieces == 2 else first.at[0] if pieces == 8 else core.at[0]

    def push(k, to, s, r, *at):
        def body(i, layer, piece):
            block = out[i].at[layer, *at, c, *cut(i, piece)]
            send(block, block, s, r, to)

        by_weight(k, body)

    def pass_on(k, odd, at, up):
        s = lax.rem(k, SLOTS)
        push(k, me + 2 if up else me - 2, sent.at[GATHERZ, s], grecv.at[s, at], *pair(odd, y if odd else x, at))

    def gather_own(k, odd):
        pl.when(k >= IN_VMEM * 2 * PER_LAYER)(lambda: wait(fresh.at[0], stored.at[lax.rem(k, LAST_SLOTS)]))
        wait(like(1), recv.at[NEXT, lax.rem(k, SLOTS)])
        pl.when(z < 3)(lambda: pass_on(k, odd, z, True))
        pl.when(z > 0)(lambda: pass_on(k, odd, z, False))

    def gather_z(k, odd, d):
        s = lax.rem(k, SLOTS)

        @pl.when(z - d >= 0)
        def _():
            wait(like(2), grecv.at[s, z - d])
            if d < 3:
                pl.when(z < 3)(lambda: pass_on(k, odd, z - d, True))

        @pl.when(z + d <= 3)
        def _():
            wait(like(2), grecv.at[s, z + d])
            if d < 3:
                pl.when(z > 0)(lambda: pass_on(k, odd, z + d, False))

    def gather_first(k, odd):
        s = lax.rem(k, SLOTS)
        push(k, across[odd], sent.at[GATHER1, s], recv.at[GATHER1, s], *pair(odd, y if odd else x, every))

    def gather_core(k, odd):
        s = lax.rem(k, SLOTS)
        wait(like(8), recv.at[GATHER1, s])
        push(k, other, sent.at[GATHER0, s], recv.at[GATHER0, s], every, every, every)

    def sent_first(k, odd):
        s = lax.rem(k, SLOTS)
        wait(core.at[0], sent.at[CORE, s])
        wait(first.at[0], sent.at[FIRST, s])

    def sent_sums(k, odd):
        s = lax.rem(k, SLOTS)
        wait(zs.at[0, pl.ds(0, 3)], sent.at[SUMZ, s])
        wait(last.at[0], sent.at[LAST, s])

    def end(k, odd):
        s = lax.rem(k, SLOTS)
        wait(like(16), recv.at[GATHER0, s])
        wait(like(1), sent.at[NEXT, s])
        pl.when(jnp.logical_or(z == 0, z == 3))(lambda: wait(like(2), sent.at[GATHERZ, s]))
        pl.when(jnp.logical_and(z > 0, z < 3))(lambda: wait(like(10), sent.at[GATHERZ, s]))
        wait(like(8), sent.at[GATHER1, s])
        wait(like(16), sent.at[GATHER0, s])

    def stage(t, half, offset, body):
        k = t - offset
        pl.when(jnp.logical_and(k >= 0, k < CHUNKS))(functools.partial(body, k, (half - offset) % 2) if isinstance(offset, int) else functools.partial(body, k))

    def tick(t, half):
        at = functools.partial(stage, t, half)
        at(END, end)
        at(G0, gather_core)
        for d in (3, 2, 1):
            at(GZ + d * LZ, functools.partial(gather_z, d=d))
        at(G1, gather_first)
        at(GZ, gather_own)
        at(NEW, update)
        at(FIN + 3, sent_sums)
        at(T + 2, sent_first)
        at(FIN, finish)
        at(T, sum_first)
        at(T + LZ * z, functools.partial(hop, up=True))
        at(T + LZ * (3 - z), functools.partial(hop, up=False))
        at(S1, first_axis)
        at(0, start)

    @pl.loop(0, (CHUNKS + END + 1) // 2)
    def _(i):
        tick(2 * i, 0)

        @pl.when(i == 0)
        def _():
            for one in loads:
                one.start()

        tick(2 * i + 1, 1)


def put(*refs):
    copies = [pltpu.make_async_copy(refs[i], refs[6 + i], refs[12].at[i]) for i in range(6)]
    for one in copies:
        one.start()
    for one in copies:
        one.wait()


def solution(mesh):
    n = (UNITS, 16, UNIT)

    def step(*arrays):
        g, w, m, v = (arrays[i : i + 3] for i in (0, 3, 6, 9))
        shapes = [one.shape for one in w]
        g = [one.reshape(2, 2, 2, 4, 2, one.shape[2] // 32, one.shape[3]) for one in g]
        w = [one.reshape(2, 32, one.shape[1] // 32, one.shape[2]) for one in w]
        results = pl.pallas_call(
            kernel,
            name="step",
            in_specs=[pl.BlockSpec(memory_space=pltpu.HBM)] * 12,
            out_specs=[pl.BlockSpec(memory_space=pltpu.HBM if IN_VMEM <= i < 3 else pltpu.VMEM) for i in range(9)],
            out_shape=[pltpu.VMEM(one.shape, BF16) if i < IN_VMEM else jax.ShapeDtypeStruct(one.shape, BF16) for i, one in enumerate(g)]
            + [pltpu.VMEM(one.shape, F32) for one in (*m, *v)],
            scratch_shapes=[
                pltpu.VMEM((OWN, 2, 2, 4, *n), BF16),
                pltpu.VMEM((CORE_SLOTS, 2, 2, 4, *n), BF16),
                pltpu.VMEM((FIRST_SLOTS, 2, 4, *n), BF16),
                pltpu.VMEM((Z_SLOTS, 5, 2, *n), BF16),
                pltpu.VMEM((LAST_SLOTS, *n), BF16),
                pltpu.VMEM((LAST_SLOTS, *n), BF16),
                pltpu.VMEM((LAST_SLOTS, *n), BF16),
                pltpu.VMEM((SUMS, 4, 2, *n), F32),
                pltpu.VMEM((2, *n), F32),
                *(pltpu.VMEM(one.shape, BF16) for one in m),
                pltpu.SemaphoreType.DMA((9,)),
                pltpu.SemaphoreType.DMA((OWN,)),
                pltpu.SemaphoreType.DMA((6, SLOTS)),
                pltpu.SemaphoreType.DMA((SLOTS, 5)),
                pltpu.SemaphoreType.DMA((SLOTS, 4)),
                pltpu.SemaphoreType.DMA((8, SLOTS)),
                pltpu.SemaphoreType.DMA((LAST_SLOTS,)),
            ],
            compiler_params=pltpu.CompilerParams(has_side_effects=True, vmem_limit_bytes=VMEM_MIB * 2**20),
        )(*g, *w, *m, *v)
        moments = pl.pallas_call(
            put,
            name="put",
            in_specs=[pl.BlockSpec(memory_space=pltpu.VMEM)] * 6,
            out_specs=[pl.BlockSpec(memory_space=pl.ANY)] * 6,
            out_shape=[jax.ShapeDtypeStruct(one.shape, one.dtype) for one in results[3:]],
            scratch_shapes=[pltpu.SemaphoreType.DMA((6,))],
            compiler_params=pltpu.CompilerParams(vmem_limit_bytes=2**20),
        )(*results[3:])
        return (*(one.reshape(shape) for one, shape in zip(results[:3], shapes, strict=True)), *moments)

    all_of, cut = P(None, None, None), P(None, "dp", None)
    return jax.shard_map(
        step,
        mesh=mesh,
        in_specs=(P(("rep", "dp"), None, None, None),) * 3 + (all_of,) * 3 + (cut,) * 6,
        out_specs=(P("rep", None, None),) * 3 + (P("rep", "dp", None),) * 6,
        check_vma=False,
    )
```

time: 961 us -> 371 us (0.39)
  waiting for transfers between devices: 902 us -> 0 us
  Pallas kernels: 0 us -> 347 us
  between operations: 14.2 us -> 0.69 us
  local copies, waits for them, and re-layouts: 34.1 us -> 23.2 us
  other arithmetic: 9.87 us -> 0.01 us
    reduce_scatter x3 -> x0, waiting for transfers between devices: 556 us -> none  [step(): lax.psum_scatter(t[0], 'dp', scatter_dimension=1, tiled=True)]
    pallas_call x0 -> x2, Pallas kernels: none -> 347 us  [the longest x1 344 us: step(): pl.pallas_call(kernel, name='step', in_specs=[pl.BlockSpec(memory_space=p...]
    all_gather x3 -> x0, waiting for transfers between devices: 344 us -> none  [step(): whole = [lax.all_gather(one[0], 'dp', axis=1, tiled=True) for one in new]]
    unnamed x19 -> x11, local copies, waits for them, and re-layouts: 34.1 us -> 23.2 us
    convert_element_type x3 -> x0, other arithmetic: 9.87 us -> none  [adamw(): return ((w - 0.02 * step).astype(jnp.bfloat16), m, v)]
  transfers between devices with their start and end apart: 6 -> 0, of which waited for: 6 -> 0; matrix products, arithmetic and copies ran while one was open for 1% -> 0% of each run, Pallas kernels for 0% -> 0%
where the time goes in v3:
time: 371 us
  Pallas kernels  347 us (94%)
  local copies, waits for them, and re-layouts  23.2 us (6%)
    pallas_call x1, Pallas kernels, step(): pl.pallas_call(kernel, name='step', in_specs=[pl.BlockSpec(memory_space=p...  344 us
    unnamed x11, local copies, waits for them, and re-layouts  23.2 us

profile of v3, /device:TPU:0, one launch (start us, length us, event | category | flops | bytes accessed | tf_op | source)
XLA Modules:
  0.0 370.7 jit_solution(9853017800478834655)
XLA Ops:
  0.6 343.6 %step.1 = (bf16[2,2,2,4,2,16,8192]{6,5,4,3,2,1,0:T(8,128)(2,1)S(1)}, bf16[2,2,2,4,2,16,8192]{6,5,4,3,2,1,0:T(8,128)(2,1)S(1)}, bf16[2,2,2,4,2,256,512]{6,5,4,3,2...) custom-call(bf16[2,2,2,4,2,16,8192]{6,5,4,3,2,1,0:T(8,128)(2,1)} %bi, ...), custom_call_target="tpu_custom_call" | custom-call | tf_op jit(solution)/shard_map/step/pallas_call | solution.py:297
  344.2 6.2 %copy.24 = bf16[2,512,8192]{2,1,0:T(8,128)(2,1)} copy(bf16[2,512,8192]{2,1,0:T(8,128)(2,1)S(1)} %bitcast.10) | data formatting | bytes 33554432
  350.4 0.0 slice-start
  350.4 0.0 slice-start.1
  350.4 0.0 slice-start.2
  350.4 0.0 slice-start.3
  350.4 8.5 %copy.25 = bf16[2,512,8192]{2,1,0:T(8,128)(2,1)} copy(bf16[2,512,8192]{2,1,0:T(8,128)(2,1)S(1)} %bitcast.9) | data formatting | bytes 33554432
  358.9 3.2 put.1
  362.1 0.0 slice-done
  362.1 0.0 slice-done.1
  362.1 1.2 slice-done.2
  363.3 1.2 slice-done.3
  364.5 6.2 %copy.26 = bf16[2,8192,512]{2,1,0:T(8,128)(2,1)} copy(bf16[2,8192,512]{2,1,0:T(8,128)(2,1)S(1)} %bitcast.19) | data formatting | bytes 33554432
  (1 shorter events, 0.0 us)
Async XLA Ops:
  350.4 11.7 %slice-start = ((s8[16777216]{0:T(1024)(128)(4,1)}), s8[4194304]{0:T(1024)(128)(4,1)S(1)}, s32[]{:S(2)}) async-start(s8[16777216]{0:T(1024)(128)(4,1)} %bitcast.17), calls=%async_computation | async-start | bytes 8388608
  350.4 11.7 %slice-start.1 = ((s8[16777216]{0:T(1024)(128)(4,1)}), s8[4194304]{0:T(1024)(128)(4,1)S(1)}, s32[]{:S(2)}) async-start(s8[16777216]{0:T(1024)(128)(4,1)} %bitcast.17), calls=%async_computation.1 | async-start | bytes 8388608
  350.4 12.9 %slice-start.2 = ((s8[16777216]{0:T(1024)(128)(4,1)}), s8[4194304]{0:T(1024)(128)(4,1)S(1)}, s32[]{:S(2)}) async-start(s8[16777216]{0:T(1024)(128)(4,1)} %bitcast.17), calls=%async_computation.2 | async-start | bytes 8388608
  350.4 14.1 %slice-start.3 = ((s8[16777216]{0:T(1024)(128)(4,1)}), s8[4194304]{0:T(1024)(128)(4,1)S(1)}, s32[]{:S(2)}) async-start(s8[16777216]{0:T(1024)(128)(4,1)} %bitcast.17), calls=%async_computation.3 | async-start | bytes 8388608

commit v4 on v3

--- a/solution.py
+++ b/solution.py
@@ -84,7 +84,7 @@
         wait(core.at[e], recv.at[CORE, s])
         wait(own.at[o], local.at[o])
 
-        @pl.loop(0, 4)
+        @pl.loop(0, 4, unroll=True)
         def _(n):
             at = pair(odd, p, n)
             core[e, *at] = (own[o, *at].astype(F32) + core[e, *at].astype(F32)).astype(BF16)
@@ -96,7 +96,7 @@
         p = y if odd else x
         wait(first.at[f], recv.at[FIRST, s])
 
-        @pl.loop(0, 4)
+        @pl.loop(0, 4, unroll=True)
         def _(n):
             at = pair(odd, p, n)
             sums[b, n] = own[o, *at].astype(F32) + core[e, *at].astype(F32) + first[f, :, n].astype(F32)
@@ -251,7 +251,6 @@
     def tick(t, half):
         at = functools.partial(stage, t, half)
         at(END, end)
-        at(G0, gather_core)
         for d in (3, 2, 1):
             at(GZ + d * LZ, functools.partial(gather_z, d=d))
         at(G1, gather_first)
@@ -264,6 +263,7 @@
         at(T + LZ * z, functools.partial(hop, up=True))
         at(T + LZ * (3 - z), functools.partial(hop, up=False))
         at(S1, first_axis)
+        at(G0, gather_core)
         at(0, start)
 
     @pl.loop(0, (CHUNKS + END + 1) // 2)

time: 371 us -> 370 us (level)
  no operation moved by 1% of the time
where the time goes in v4:
time: 370 us
  Pallas kernels  346 us (94%)
  local copies, waits for them, and re-layouts  23.2 us (6%)
    pallas_call x1, Pallas kernels, step(): pl.pallas_call(kernel, name='step', in_specs=[pl.BlockSpec(memory_space=p...  343 us
    unnamed x11, local copies, waits for them, and re-layouts  23.2 us

profile of v4, /device:TPU:0, one launch (start us, length us, event | category | flops | bytes accessed | tf_op | source)
XLA Modules:
  0.0 369.6 jit_solution(18052385096697563101)
XLA Ops:
  0.6 342.5 %step.1 = (bf16[2,2,2,4,2,16,8192]{6,5,4,3,2,1,0:T(8,128)(2,1)S(1)}, bf16[2,2,2,4,2,16,8192]{6,5,4,3,2,1,0:T(8,128)(2,1)S(1)}, bf16[2,2,2,4,2,256,512]{6,5,4,3,2...) custom-call(bf16[2,2,2,4,2,16,8192]{6,5,4,3,2,1,0:T(8,128)(2,1)} %bi, ...), custom_call_target="tpu_custom_call" | custom-call | tf_op jit(solution)/shard_map/step/pallas_call | solution.py:297
  343.2 6.2 %copy.24 = bf16[2,512,8192]{2,1,0:T(8,128)(2,1)} copy(bf16[2,512,8192]{2,1,0:T(8,128)(2,1)S(1)} %bitcast.10) | data formatting | bytes 33554432
  349.4 0.0 slice-start
  349.4 0.0 slice-start.1
  349.4 0.0 slice-start.2
  349.4 0.0 slice-start.3
  349.4 8.5 %copy.25 = bf16[2,512,8192]{2,1,0:T(8,128)(2,1)} copy(bf16[2,512,8192]{2,1,0:T(8,128)(2,1)S(1)} %bitcast.9) | data formatting | bytes 33554432
  357.9 3.2 put.1
  361.1 0.0 slice-done
  361.1 0.0 slice-done.1
  361.1 1.2 slice-done.2
  362.3 1.2 slice-done.3
  363.5 6.2 %copy.26 = bf16[2,8192,512]{2,1,0:T(8,128)(2,1)} copy(bf16[2,8192,512]{2,1,0:T(8,128)(2,1)S(1)} %bitcast.19) | data formatting | bytes 33554432
  (1 shorter events, 0.0 us)
Async XLA Ops:
  349.4 11.7 %slice-start = ((s8[16777216]{0:T(1024)(128)(4,1)}), s8[4194304]{0:T(1024)(128)(4,1)S(1)}, s32[]{:S(2)}) async-start(s8[16777216]{0:T(1024)(128)(4,1)} %bitcast.17), calls=%async_computation | async-start | bytes 8388608
  349.4 11.7 %slice-start.1 = ((s8[16777216]{0:T(1024)(128)(4,1)}), s8[4194304]{0:T(1024)(128)(4,1)S(1)}, s32[]{:S(2)}) async-start(s8[16777216]{0:T(1024)(128)(4,1)} %bitcast.17), calls=%async_computation.1 | async-start | bytes 8388608
  349.4 12.9 %slice-start.2 = ((s8[16777216]{0:T(1024)(128)(4,1)}), s8[4194304]{0:T(1024)(128)(4,1)S(1)}, s32[]{:S(2)}) async-start(s8[16777216]{0:T(1024)(128)(4,1)} %bitcast.17), calls=%async_computation.2 | async-start | bytes 8388608
  349.4 14.1 %slice-start.3 = ((s8[16777216]{0:T(1024)(128)(4,1)}), s8[4194304]{0:T(1024)(128)(4,1)S(1)}, s32[]{:S(2)}) async-start(s8[16777216]{0:T(1024)(128)(4,1)} %bitcast.17), calls=%async_computation.3 | async-start | bytes 8388608
